TPU v7x, 32 devices: a whole 2x2x4 slice. The times are simulated.
32 devices in a mesh: member: 8 (over z, core), space: 4 (over y, x).
Axes of the slice: x: 2, y: 2, z: 4, core: 2. Of those that a mesh axis runs over, the one named last changes fastest.
Arguments:
- weather: bfloat16 [8, 84, 64, 1440], P('member', None, 'space'), may hold values from -6 to 6
- coefficients: int32 [8, 84, 2, 364, 361], P('member', None, None, 'space'), may hold values from -1073741824 to 1073741823
- channel_scale: float32 [84], replicated, may hold values from 0.3 to 3
Outputs:
- perturbed: bfloat16 [8, 84, 64, 1440], P('member', None, 'space')
All inputs are finite; a program needn't handle non-finite values.
Results may differ from a plain program's by a relative error of at most 0.007.
Values may be sent and summed in bfloat16 or wider, within the bound.
A program may use at most 192 MiB of HBM per device.

v0:
```python
import math

import jax
import jax.numpy as jnp
from jax import lax
from jax.sharding import PartitionSpec as P


def diagonal_log(order_count):
    steps_up = jnp.arange(1, order_count, dtype=jnp.int32).astype(jnp.float32)
    terms = 0.5 * jnp.log((2.0 * steps_up + 1.0) / (2.0 * steps_up))
    return jnp.concatenate([jnp.zeros((1,), jnp.float32), jnp.cumsum(terms)])


def legendre_table(orders, colatitude, order_logs, degree_count):
    order_values = orders.astype(jnp.float32)[:, None]
    cosine = jnp.cos(colatitude)[None, :]
    sine_values = jnp.sin(colatitude)[None, :]
    diagonal = jnp.exp(
        order_logs[:, None] - 0.5 * math.log(4.0 * math.pi) + order_values * jnp.log(sine_values)
    )
    block_size = 16
    turn_count = (degree_count + block_size - 1) // block_size
    order_square = order_values * order_values

    def advance(carry, turn_index):
        older_row, newer_row = carry
        produced = []
        for inner_step in range(block_size):
            degree = (turn_index * block_size + inner_step).astype(jnp.float32)
            degree_square = degree * degree
            prior = degree - 1.0
            factor_up = jnp.sqrt(
                jnp.maximum(4.0 * degree_square - 1.0, 1.0)
                / jnp.maximum(degree_square - order_square, 1.0)
            )
            factor_down = jnp.sqrt(
                jnp.maximum(prior * prior - order_square, 0.0)
                / jnp.maximum(4.0 * prior * prior - 1.0, 1.0)
            )
            next_row = factor_up * (cosine * newer_row - factor_down * older_row)
            next_row = jnp.where(
                degree < order_values, 0.0, jnp.where(degree == order_values, diagonal, next_row)
            )
            produced.append(next_row)
            older_row, newer_row = (newer_row, next_row)
        return ((older_row, newer_row), jnp.stack(produced))

    empty = jnp.zeros_like(diagonal)
    carried, stacked = lax.scan(advance, (empty, empty), jnp.arange(turn_count, dtype=jnp.int32))
    return stacked.reshape(turn_count * block_size, orders.shape[0], colatitude.shape[0])[
        :degree_count
    ]


def spectral_values(coefficients, orders):
    degree_count = coefficients.shape[-1]
    degrees = jnp.arange(degree_count, dtype=jnp.int32)
    keep = degrees[None, :] >= orders[:, None]
    factor = math.sqrt(3.0) * math.sqrt(4.0 * math.pi) / degree_count * 2.0 ** (-30)
    values = coefficients.astype(jnp.float32) * factor
    return jnp.where(keep, values, 0.0).astype(jnp.bfloat16)


def fourier_basis(order_count, lon_count):
    orders = jnp.arange(order_count, dtype=jnp.int32)
    columns = jnp.arange(lon_count, dtype=jnp.int32)
    phases = orders[:, None] * columns[None, :] % lon_count
    angles = 2.0 * math.pi / lon_count * phases.astype(jnp.float32)
    weights = jnp.where(orders == 0, 1.0, math.sqrt(2.0)).astype(jnp.float32)[:, None]
    return jnp.stack([weights * jnp.cos(angles), weights * jnp.sin(angles)]).astype(jnp.bfloat16)


def local(weather, coefficients, channel_scale):
    group_count = lax.axis_size("member")
    band_count = lax.axis_size("space")
    member_local, channels, rows_local, lon_count = weather.shape
    order_local = coefficients.shape[3]
    degree_count = coefficients.shape[4]
    order_count = order_local * band_count
    lat_count = rows_local * band_count
    lat_local = rows_local // group_count
    member_count = member_local * group_count
    first_order = lax.axis_index("space") * order_local
    orders = first_order + jnp.arange(order_local, dtype=jnp.int32)
    order_logs = lax.dynamic_slice_in_dim(diagonal_log(order_count), first_order, order_local)
    row_first = (lon_count // 2 + 1 - lat_count) // 2
    colatitude = (
        math.pi
        * (row_first + jnp.arange(lat_count, dtype=jnp.int32)).astype(jnp.float32)
        / (lon_count // 2)
    )
    legendre = legendre_table(orders, colatitude, order_logs, degree_count).astype(jnp.bfloat16)
    spectral = spectral_values(coefficients, orders)
    fourier = jnp.einsum(
        "ecpml,lmt->ectpm", spectral, legendre, preferred_element_type=jnp.float32
    ).astype(jnp.bfloat16)
    fourier = fourier.reshape(
        member_local, channels, band_count, group_count, lat_local, 2, order_local
    )
    basis = fourier_basis(order_count, lon_count).reshape(2 * order_count, lon_count)
    scale_wide = channel_scale[None, :, None, None, None]
    pieces = weather.reshape(member_local, channels, group_count, lat_local, lon_count)
    own_rows = lax.all_to_all(fourier, "space", split_axis=2, concat_axis=6, tiled=True)
    own_flat = own_rows.reshape(member_local * channels * rows_local, 2 * order_count)
    own_noise = jnp.dot(own_flat, basis, preferred_element_type=jnp.float32).astype(jnp.bfloat16)
    own_wide = lax.optimization_barrier(own_noise).astype(jnp.float32)
    own_wide = own_wide.reshape(member_local, channels, group_count, lat_local, lon_count)
    local_total = jnp.sum(own_wide, axis=0)
    ensemble_total = lax.psum(local_total.astype(jnp.bfloat16), "member").astype(jnp.float32)
    centred = own_wide - (ensemble_total / member_count)[None]
    returned = (pieces.astype(jnp.float32) + scale_wide * centred).astype(jnp.bfloat16)
    return returned.reshape(member_local, channels, rows_local, lon_count)


def solution(mesh):
    return jax.shard_map(
        local,
        mesh=mesh,
        in_specs=(P("member", None, "space", None), P("member", None, None, "space", None), P()),
        out_specs=P("member", None, "space", None),
        check_vma=False,
    )
```

profile of v0, /device:TPU:0, one launch (start us, length us, event | category | flops | bytes accessed | tf_op | source)
XLA Modules:
  0.0 421.5 jit_solution(12412747525541009677)
XLA Ops:
  7.4 162.3 %while.21 = (s32[]{:T(128)}, f32[91,64]{1,0:T(8,128)S(1)}, f32[91,64]{1,0:T(8,128)S(1)}, bf16[23,16,91,64]{3,2,1,0:T(8,128)(2,1)}, s32[23]{0:T(128)S(1)}, /*inde...) while((s32[]{:T(128)}, f32[91,64]{1,0:T(8,128)S(1)}, ...), condition=%wide.region_3.4_spmd.clone.clone.clone.clone, body=%wide.region_2.3_spmd.clone.clone.clone.clone.sunk | while | flops 1754866 | bytes 3612135 | solution.py:50
  13.7 0.8 bitcast_dynamic-update-slice_fusion.50
  27.8 0.8 bitcast_dynamic-update-slice_fusion.50
  56.0 0.8 bitcast_dynamic-update-slice_fusion.50
  70.1 0.8 bitcast_dynamic-update-slice_fusion.50
  77.2 0.8 bitcast_dynamic-update-slice_fusion.50
  98.3 0.8 bitcast_dynamic-update-slice_fusion.50
  119.5 0.8 bitcast_dynamic-update-slice_fusion.50
  126.5 0.8 bitcast_dynamic-update-slice_fusion.50
  147.7 0.8 bitcast_dynamic-update-slice_fusion.50
  154.8 0.8 bitcast_dynamic-update-slice_fusion.50
  161.9 0.8 bitcast_dynamic-update-slice_fusion.50
  169.0 0.8 bitcast_dynamic-update-slice_fusion.50
  169.7 8.5 %slice.18 = bf16[361,91,64]{2,1,0:T(8,128)(2,1)} slice(bf16[368,91,64]{2,1,0:T(8,128)(2,1)} %bitcast.343), slice={[0:361], [0:91], [0:64]} | slice | bytes 8409856 | tf_op jit(solution)/shard_map/slice | solution.py:51
  178.3 12.7 %copy.22 = bf16[361,91,64]{0,2,1:T(8,128)(2,1)} copy(bf16[361,91,64]{2,1,0:T(8,128)(2,1)} %slice.18) | data formatting | bytes 8409856
  191.1 16.9 %fusion.44 = bf16[84,2,91,361]{3,1,2,0:T(2,128)(2,1)S(1)} fusion(s32[1,84,2,91,361]{4,2,3,1,0:T(2,128)} %param.6, pred[91,361]{1,0:T(8,128)(4,1)S(1)} %iota_compare_fusion), kind=kLoop, calls=%fused_computation.127 | loop fusion | flops 22075872 | bytes 33146660 | tf_op jit(solution)/shard_map/reshape.15
  208.0 7.7 %fusion.51 = bf16[91,64,84,2]{2,1,3,0:T(8,128)(2,1)} fusion(bf16[84,2,91,361]{3,1,2,0:T(2,128)(2,1)S(1)} %fusion.44, bf16[361,91,64]{0,2,1:T(8,128)(2,1)S(1)} %copy-done), kind=kOutput, calls=%fused_computation.141 | convolution fusion | flops 707406336 | bytes 17199728 | tf_op jit(solution)/shard_map/ecpml,lmt->ectpm/dot_general | solution.py:95
  215.7 11.3 %copy.16 = bf16[1,84,4,8,2,2,91]{6,5,4,3,1,0,2:T(2,128)(2,1)} copy(bf16[1,84,4,8,2,2,91]{1,4,3,2,5,6,0:T(2,128)(2,1)} %bitcast.341) | data formatting | bytes 3913728 | tf_op jit(solution)/shard_map/reshape | solution.py:98
  227.0 5.2 %all-to-all-start = ((bf16[1,84,4,8,2,2,91]{6,5,4,3,1,0,2:T(2,128)(2,1)}), bf16[1,84,4,8,2,2,91]{6,5,4,3,1,0,2:T(2,128)(2,1)S(1)}, u32[]{:S(2)}, u32[]{:S(2)}) async-start(bf16[1,84,4,8,2,2,91]{6,5,4,3,1,0,2:T(2,128)(2,1)} %copy.16), calls=%async_computation | async-start | bytes 5505024 | tf_op jit(solution)/shard_map/all_to_all | solution.py:104
  232.2 9.8 %multiply_convert_fusion.1 = (bf16[1,364,1440]{2,1,0:T(8,128)(2,1)S(1)}, bf16[1,364,1440]{2,1,0:T(8,128)(2,1)S(1)}) fusion(f32[364]{0:T(512)S(1)} %fusion.58), kind=kLoop, calls=%fused_computation.136 | loop fusion | flops 6814080 | bytes 2098096 | tf_op jit(solution)/shard_map/convert.2
  242.0 1.6 pad_maximum_fusion
  243.6 4.1 convert_element_type.300
  247.7 16.4 %all-to-all-done = bf16[1,84,4,8,2,2,91]{6,5,4,3,1,0,2:T(2,128)(2,1)S(1)} async-done(((bf16[1,84,4,8,2,2,91]{6,5,4,3,1,0,2:T(2,128)(2,1)}), bf16[1,84,4,8,2,2,91]{6,5,4,3,1,0,2:T(2,128)(2,1)S(1)}, u32[]{:S(2)}, u32[]{:S(2)}) %all-to-all-start) | async-done | bytes 1956896 | tf_op jit(solution)/shard_map/all_to_all | solution.py:104
  264.1 5.1 %copy.17 = bf16[1,84,1,8,2,2,4,91]{7,6,5,4,3,1,2,0:T(4,128)(2,1)} copy(bf16[1,84,1,8,2,2,4,91]{7,5,4,3,1,6,2,0:T(2,128)(2,1)S(1)} %bitcast.342) | data formatting | bytes 3913728 | tf_op jit(solution)/shard_map/all_to_all | solution.py:104
  269.2 6.3 %reshape.1190 = bf16[1344,728]{1,0:T(8,128)(2,1)} reshape(bf16[1,84,1,8,2,2,4,91]{7,6,5,4,3,1,2,0:T(4,128)(2,1)} %copy.17) | data formatting | bytes 3913728 | tf_op jit(solution)/shard_map/reshape | solution.py:105
  275.5 7.0 %convolution_convert_fusion = bf16[1344,1440]{0,1:T(8,128)(2,1)} fusion(bf16[1344,728]{1,0:T(8,128)(2,1)} %reshape.1190, bf16[728,1440]{1,0:T(8,128)(2,1)S(1)} %copy-done.1), kind=kOutput, calls=%fused_computation.129 | convolution fusion | flops 2819819520 | bytes 7924224 | tf_op jit(solution)/shard_map/dot_general | solution.py:106
  282.5 6.3 %copy.18 = bf16[1344,1440]{1,0:T(8,128)(2,1)} copy(bf16[1344,1440]{0,1:T(8,128)(2,1)} %convolution_convert_fusion) | data formatting | bytes 7741440 | tf_op jit(solution)/shard_map/optimization_barrier | solution.py:107
  288.7 9.2 %reshape.1191 = bf16[84,8,2,1440]{3,2,1,0:T(2,128)(2,1)} reshape(bf16[1344,1440]{1,0:T(8,128)(2,1)} %copy.18) | data formatting | bytes 7741440 | tf_op jit(solution)/shard_map/reshape | solution.py:108
  297.9 9.9 %reshape.1194 = f32[84,8,2,1440]{3,2,1,0:T(2,128)} reshape(bf16[1,84,16,1440]{3,2,1,0:T(8,128)(2,1)} %param.5) | data formatting | bytes 11612160 | tf_op jit(solution)/shard_map/convert_element_type | solution.py:112
  307.9 85.9 %all-reduce.3.cloned.1.call-done = bf16[84,8,2,1440]{3,2,1,0:T(2,128)(2,1)} async-done(((bf16[84,8,2,1440]{3,2,1,0:T(2,128)(2,1)}), bf16[84,8,2,1440]{3,2,1,0:T(2,128)(2,1)}) %all-reduce.3.cloned.1.call-update) | async-done | bytes 3870736 | tf_op jit(solution)/shard_map/psum | solution.py:110
  393.8 11.5 %add_convert_fusion = bf16[84,8,2,1440]{3,2,1,0:T(2,128)(2,1)} fusion(f32[84,8,2,1440]{3,2,1,0:T(2,128)} %reshape.1194, bf16[84,8,2,1440]{3,2,1,0:T(2,128)(2,1)} %all-reduce.3.cloned.1.call-done, bf16[84,8,2,1440]{3,2,1,0:T(2,128)(2,1)} %reshape.1191, f32[84]{0:T(128)S(1)} %copy-done.2), kind=kLoop, calls=%fused_computation.128 | loop fusion | flops 13547520 | bytes 19353936 | tf_op jit(solution)/shard_map/convert_element_type | solution.py:112
  405.3 9.4 %reshape.1193 = bf16[1,84,16,1440]{3,2,1,0:T(8,128)(2,1)} reshape(bf16[84,8,2,1440]{3,2,1,0:T(2,128)(2,1)} %add_convert_fusion) | data formatting | bytes 7741440 | tf_op jit(solution)/shard_map/reshape | solution.py:113
  (1186 shorter events, 126.8 us)
Async XLA Ops:
  191.1 16.9 %copy-start = (bf16[361,91,64]{0,2,1:T(8,128)(2,1)S(1)}, bf16[361,91,64]{0,2,1:T(8,128)(2,1)}, u32[]{:S(2)}) copy-start(bf16[361,91,64]{0,2,1:T(8,128)(2,1)} %copy.22) | copy-start | bytes 12614788
  227.0 37.1 %all-to-all-start = ((bf16[1,84,4,8,2,2,91]{6,5,4,3,1,0,2:T(2,128)(2,1)}), bf16[1,84,4,8,2,2,91]{6,5,4,3,1,0,2:T(2,128)(2,1)S(1)}, u32[]{:S(2)}, u32[]{:S(2)}) async-start(bf16[1,84,4,8,2,2,91]{6,5,4,3,1,0,2:T(2,128)(2,1)} %copy.16), calls=%async_computation | async-start | bytes 5505024 | tf_op jit(solution)/shard_map/all_to_all | solution.py:104
  232.2 161.6 %all-reduce.3.cloned.1.call-start = ((), (), s32[]{:S(2)}) async-start(), calls=%async_computation.1 | async-start | bytes 8257536 | tf_op jit(solution)/shard_map/psum | solution.py:110
  269.2 6.4 %copy-start.1 = (bf16[728,1440]{1,0:T(8,128)(2,1)S(1)}, bf16[728,1440]{1,0:T(8,128)(2,1)}, u32[]{:S(2)}) copy-start(bf16[728,1440]{1,0:T(8,128)(2,1)} %convert_element_type.300) | copy-start | bytes 6289924
  297.9 95.9 %copy-start.2 = (f32[84]{0:T(128)S(1)}, f32[84]{0:T(128)}, u32[]{:S(2)}) copy-start(f32[84]{0:T(128)} %param.7) | copy-start | bytes 1012
Sparse Core Ops, SparseCore 0:
  298.0 95.7 all-reduce.2
where the time goes:
time: 423 us; the launch traced here: 422 us
  other arithmetic  143 us (34%)
  local copies, waits for them, and re-layouts  116 us (27%)
  waiting for transfers between devices  102 us (24%)
  loops' own time  26.9 us (6%)
  matrix products  14.7 us (3%)
  between operations  13.5 us (3%)
  starting transfers between devices  5.19 us (1%)
    while x345, other arithmetic  86.7 us
    psum x1, waiting for transfers between devices, local(): lax.psum(local_total.astype(jnp.bfloat16), 'member').astype(jnp.float32)  85.9 us
    another operation x5, other arithmetic  27.1 us
    another operation x1, loops' own time, legendre_table(): lax.scan(advance, (empty, empty), jnp.arange(turn_count, dtype=jnp.int32))  26.9 us
    dynamic_update_slice x23, local copies, waits for them, and re-layouts, legendre_table(): lax.scan(advance, (empty, empty), jnp.arange(turn_count, dtype=jnp.int32))  18.1 us
    all_to_all x1, waiting for transfers between devices, local(): lax.all_to_all(fourier, 'space', split_axis=2, concat_axis=6, tiled=True)  16.4 us
    dynamic_slice x23, local copies, waits for them, and re-layouts, legendre_table(): lax.scan(advance, (empty, empty), jnp.arange(turn_count, dtype=jnp.int32))  15.2 us
    unnamed x7, local copies, waits for them, and re-layouts  12.7 us
  transfers between devices with their start and end apart: 2, of which 2 were waited for; matrix products, arithmetic and copies ran while one was open for 6% of the time, Pallas kernels for 0%

commit v1 on v0

v1 whole, which is shorter than its diff:
```python
import functools
import math

import jax
import jax.numpy as jnp
from jax import lax
from jax.experimental import pallas as pl
from jax.experimental.pallas import tpu as pltpu
from jax.sharding import PartitionSpec as P


def round_up(value, step):
    return (value + step - 1) // step * step


def diagonal_log(order_count):
    steps_up = jnp.arange(1, order_count, dtype=jnp.int32).astype(jnp.float32)
    terms = 0.5 * jnp.log((2.0 * steps_up + 1.0) / (2.0 * steps_up))
    return jnp.concatenate([jnp.zeros((1,), jnp.float32), jnp.cumsum(terms)])


def synthesis_kernel(block, pitch, order_ref, cosine_ref, diagonal_ref, spectral_ref, out_ref, table):
    half, lanes = order_ref.shape
    degrees = spectral_ref.shape[-1]

    @pl.when(pl.program_id(0) == 0)
    def build():
        order = order_ref[...]
        order_square = order * order
        cosine = jnp.broadcast_to(cosine_ref[...], (half, lanes))
        diagonal = diagonal_ref[...]

        def advance(step, carry):
            older, newer, down = carry
            degree = step.astype(jnp.float32)
            wide = jnp.full((half, lanes), degree, jnp.float32)
            square = wide * wide
            ratio = jnp.maximum(square - order_square, 0.25) / jnp.maximum(4.0 * square - 1.0, 1.0)
            up = lax.rsqrt(ratio)
            row = up * (cosine * newer - down * older)
            row = jnp.where(wide < order, 0.0, jnp.where(wide == order, diagonal, row))
            for tile in range(lanes // 128):
                table[pl.ds(tile * half * pitch + step, half, stride=pitch), :] = row[
                    :, tile * 128 : tile * 128 + 128
                ]
            return newer, row, ratio * up

        zero = order * 0.0
        lax.fori_loop(0, degrees, advance, (zero, zero, zero), unroll=4)

    first = pl.program_id(0) * block
    rows = spectral_ref.shape[2]
    low = lax.broadcasted_iota(jnp.int32, (rows, lanes), 1) < lanes // 2
    for inner in range(block):
        tiles = []
        for tile in range(lanes // 128):
            start = pl.multiple_of((tile * half + first + inner) * pitch, 8)
            tiles.append(table[pl.ds(start, degrees), :].astype(jnp.bfloat16))
        values = jnp.concatenate(tiles, axis=1)
        both = jnp.concatenate([spectral_ref[0, inner], spectral_ref[1, inner]], axis=0)
        found = jnp.dot(both, values, preferred_element_type=jnp.float32)
        out_ref[inner] = jnp.where(low, found[:rows], found[rows:]).astype(jnp.bfloat16)


def synthesize(spectral, order_plane, cosine_row, diagonal_plane):
    pair, half, rows, degrees = spectral.shape
    lanes = order_plane.shape[1]
    block = 8
    pitch = degrees + 8
    return pl.pallas_call(
        functools.partial(synthesis_kernel, block, pitch),
        grid=(half // block,),
        out_shape=jax.ShapeDtypeStruct((half, rows, lanes), jnp.bfloat16),
        in_specs=[
            pl.BlockSpec((half, lanes), lambda i: (0, 0)),
            pl.BlockSpec((1, lanes), lambda i: (0, 0)),
            pl.BlockSpec((half, lanes), lambda i: (0, 0)),
            pl.BlockSpec((pair, block, rows, degrees), lambda i: (0, i, 0, 0)),
        ],
        out_specs=pl.BlockSpec((block, rows, lanes), lambda i: (i, 0, 0)),
        scratch_shapes=[pltpu.VMEM((lanes // 128 * half * pitch, 128), jnp.float32)],
        compiler_params=pltpu.CompilerParams(vmem_limit_bytes=60 * 1024 * 1024),
    )(order_plane, cosine_row, diagonal_plane, spectral)


def local(weather, coefficients, channel_scale):
    group_count = lax.axis_size("member")
    band_count = lax.axis_size("space")
    member_local, channels, rows_local, lon_count = weather.shape
    order_local = coefficients.shape[3]
    degree_count = coefficients.shape[4]
    order_count = order_local * band_count
    lat_count = rows_local * band_count
    member_count = member_local * group_count
    rows = member_local * channels * 2
    half = round_up(order_local, 16) // 2
    padded = 2 * half
    degrees_padded = round_up(degree_count, 128)

    first_order = lax.axis_index("space") * order_local
    slots = jnp.arange(padded, dtype=jnp.int32)
    orders = first_order + slots
    logs = jnp.pad(diagonal_log(order_count), (0, padded))
    order_logs = lax.dynamic_slice_in_dim(logs, first_order, padded)
    row_first = (lon_count // 2 + 1 - lat_count) // 2
    colatitude = (
        math.pi
        * (row_first + jnp.arange(lat_count, dtype=jnp.int32)).astype(jnp.float32)
        / (lon_count // 2)
    )
    order_values = orders.astype(jnp.float32)[:, None]
    diagonal = jnp.exp(
        order_logs[:, None]
        - 0.5 * math.log(4.0 * math.pi)
        + order_values * jnp.log(jnp.sin(colatitude))[None, :]
    )

    def pair_up(plane):
        return jnp.concatenate([plane[:half], plane[half:]], axis=1)

    order_plane = pair_up(jnp.broadcast_to(order_values, (padded, lat_count)))
    cosine_row = jnp.tile(jnp.cos(colatitude), 2)[None, :]

    degrees = jnp.arange(degree_count, dtype=jnp.int32)
    keep = degrees[None, :] >= orders[:order_local, None]
    factor = math.sqrt(3.0) * math.sqrt(4.0 * math.pi) / degree_count * 2.0 ** (-30)
    spectral = jnp.where(keep, coefficients.astype(jnp.float32) * factor, 0.0).astype(jnp.bfloat16)
    spectral = spectral.transpose(3, 0, 1, 2, 4).reshape(order_local, rows, degree_count)
    spectral = jnp.pad(
        spectral, ((0, padded - order_local), (0, 0), (0, degrees_padded - degree_count))
    ).reshape(2, half, rows, degrees_padded)
    found = synthesize(spectral, order_plane, cosine_row, pair_up(diagonal))

    found = found.reshape(half, member_local * channels, 2, 2, band_count, rows_local)
    found = found.transpose(4, 3, 2, 0, 1, 5)
    depth = padded * 2
    flat = member_local * channels * rows_local
    found = found.reshape(band_count, depth, flat)
    own = lax.all_to_all(found, "space", split_axis=0, concat_axis=0, tiled=True)

    band = jnp.arange(band_count, dtype=jnp.int32)[:, None]
    slot = slots.reshape(2, half)
    row_order = band * order_local + slots[None, :]
    real_slot = jnp.broadcast_to(slots[None, :] < order_local, row_order.shape)
    columns = jnp.arange(lon_count, dtype=jnp.int32)
    phases = row_order[:, :, None] * columns % lon_count
    angles = 2.0 * math.pi / lon_count * phases.astype(jnp.float32)
    weights = jnp.where(real_slot, jnp.where(row_order == 0, 1.0, math.sqrt(2.0)), 0.0)
    weights = weights.astype(jnp.float32)[:, :, None]
    shape = (band_count, 2, half, lon_count)
    basis = jnp.stack(
        [(weights * jnp.cos(angles)).reshape(shape), (weights * jnp.sin(angles)).reshape(shape)], axis=2
    ).astype(jnp.bfloat16)
    basis = basis.reshape(band_count * depth, lon_count)

    own = own.reshape(band_count * depth, flat)
    split = own.astype(jnp.float32).reshape(band_count * depth, member_local, -1)
    total = lax.psum(jnp.sum(split, axis=1).astype(jnp.bfloat16), "member").astype(jnp.float32)
    centred = (split - total[:, None, :] * (1.0 / member_count)).astype(jnp.bfloat16)
    centred = centred.reshape(band_count * depth, flat)
    noise = lax.dot_general(
        centred, basis, (((0,), (0,)), ((), ())), preferred_element_type=jnp.float32
    )
    noise = noise.reshape(member_local, channels, rows_local, lon_count)
    scale_wide = channel_scale[None, :, None, None]
    return (weather.astype(jnp.float32) + scale_wide * noise).astype(jnp.bfloat16)


def solution(mesh):
    return jax.shard_map(
        local,
        mesh=mesh,
        in_specs=(P("member", None, "space", None), P("member", None, None, "space", None), P()),
        out_specs=P("member", None, "space", None),
        check_vma=False,
    )
```

time: 423 us -> 221 us (0.52)
  other arithmetic: 143 us -> 35.1 us
  local copies, waits for them, and re-layouts: 116 us -> 65.1 us
  loops' own time: 26.9 us -> 0 us
  waiting for transfers between devices: 102 us -> 79.1 us
  Pallas kernels: 0 us -> 15.3 us
  matrix products: 14.7 us -> 7.17 us
    while x345 -> x0, other arithmetic: 86.7 us -> none
    psum x1, waiting for transfers between devices: 85.9 us -> 53.6 us  [local(): lax.psum(jnp.sum(split, axis=1).astype(jnp.bfloat16), 'member')]
    another operation x1 -> x0, loops' own time: 26.9 us -> none  [legendre_table(): lax.scan(advance, (empty, empty), jnp.arange(turn_count, dtype=jnp.int32))]
    reshape x5 -> x3, local copies, waits for them, and re-layouts: 36.2 us -> 12.9 us  [the longest x2 12.9 us: local(): found = found.reshape(band_count, depth, flat)]
    another operation x29 -> x5, other arithmetic: 33.6 us -> 12.7 us
    dynamic_update_slice x23 -> x0, local copies, waits for them, and re-layouts: 18.1 us -> none  [legendre_table(): lax.scan(advance, (empty, empty), jnp.arange(turn_count, dtype=jnp.int32))]
    transpose x0 -> x1, other arithmetic: none -> 16.8 us  [local(): spectral.transpose(3, 0, 1, 2, 4).reshape(order_local, rows, degree_count)]
    pallas_call x0 -> x1, Pallas kernels: none -> 15.3 us  [synthesize(): pl.pallas_call(functools.partial(synthesis_kernel, block, pitch), grid=(h...]
where the time goes in v1:
time: 221 us
  waiting for transfers between devices  79.1 us (36%)
  local copies, waits for them, and re-layouts  65.1 us (29%)
  other arithmetic  35.1 us (16%)
  Pallas kernels  15.3 us (7%)
  between operations  13.5 us (6%)
  matrix products  7.17 us (3%)
  starting transfers between devices  5.2 us (2%)
    psum x1, waiting for transfers between devices, local(): lax.psum(jnp.sum(split, axis=1).astype(jnp.bfloat16), 'member')  53.6 us
    all_to_all x1, waiting for transfers between devices, local(): lax.all_to_all(found, 'space', split_axis=0, concat_axis=0, tiled=True)  25.5 us
    transpose x1, other arithmetic, local(): spectral.transpose(3, 0, 1, 2, 4).reshape(order_local, rows, degree_count)  16.8 us
    unnamed x9, local copies, waits for them, and re-layouts  16.3 us
    pallas_call x1, Pallas kernels, synthesize(): pl.pallas_call(functools.partial(synthesis_kernel, block, pitch), grid=(h...  15.3 us
    reshape x2, local copies, waits for them, and re-layouts, local(): found = found.reshape(band_count, depth, flat)  12.9 us
    transpose x1, local copies, waits for them, and re-layouts, local(): found = found.transpose(4, 3, 2, 0, 1, 5)  11.3 us
    another operation x4, other arithmetic  11.1 us
  transfers between devices with their start and end apart: 2, of which 2 were waited for; matrix products, arithmetic and copies ran while one was open for 6% of the time, Pallas kernels for 0%

profile of v1, /device:TPU:0, one launch (start us, length us, event | category | flops | bytes accessed | tf_op | source)
XLA Modules:
  0.0 220.5 jit_solution(16218140985879516086)
XLA Ops:
  6.7 0.3 reduce-window.9
  7.0 0.1 slice.37
  7.1 0.1 slice_reduce_fusion
  7.2 0.1 add_bitcast_fusion
  7.3 0.1 select_maximum_fusion
  7.4 0.1 dynamic-slice_add_fusion
  7.5 0.1 add_exponential_fusion
  7.6 0.1 slice_bitcast_fusion.1
  7.7 0.1 iota_compare_fusion
  7.7 16.8 %fusion = bf16[91,1,84,2,361]{4,3,0,2,1:T(2,128)(2,1)S(1)} fusion(s32[1,84,2,91,361]{4,2,3,1,0:T(2,128)} %param.4, pred[91,361]{1,0:T(8,128)(4,1)S(1)} %iota_compare_fusion), kind=kLoop, calls=%fused_computation.1 | loop fusion | flops 22075872 | bytes 33146660 | tf_op jit(solution)/shard_map/transpose | solution.py:128
  24.5 2.3 %copy.18 = bf16[91,1,84,2,361]{4,0,3,2,1:T(8,128)(2,1)S(1)} copy(bf16[91,1,84,2,361]{4,3,0,2,1:T(2,128)(2,1)S(1)} %fusion) | data formatting | bytes 22075872 | tf_op jit(solution)/shard_map/transpose | solution.py:128
  26.8 15.0 %copy.27 = bf16[91,168,361]{2,1,0:T(8,128)(2,1)} copy(bf16[91,168,361]{2,0,1:T(8,128)(2,1)S(1)} %bitcast.34) | data formatting | bytes 22075872
  41.7 0.6 broadcast_in_dim_tile.3.cosine_ref
  42.4 0.7 pad_maximum_fusion.2.diagonal_ref
  43.2 0.7 pad_maximum_fusion.1.order_ref
  43.9 10.6 %pad.13.clone = bf16[96,168,384]{2,1,0:T(8,128)(2,1)} pad(bf16[91,168,361]{2,1,0:T(8,128)(2,1)} %copy.27, bf16[]{:T(256)} %constant.59.clone.1), padding=0_5x0_0x0_23 | pad | bytes 23424242 | tf_op jit(solution)/shard_map/jit(_pad)/pad | solution.py:129
  54.5 15.3 %shard_map.37 = bf16[48,168,128]{2,1,0:T(8,128)(2,1)} custom-call(f32[48,128]{1,0:T(8,128)} %pad_maximum_fusion.1.order_ref, f32[1,128]{1,0:T(1,128)} %broadcast_in_dim_tile.3.cosine_ref, f32[48,128]{1,0:T(8,128)} %pad_maximum_fusion.2.diagonal_ref, bf16[2,48,168,384]{3,2,1,0:T(8,128)(2,1)} %bitcast.33), custom_call_target="tpu_custom_call" | custom-call | tf_op jit(solution)/shard_map/pallas_call | solution.py:70
  69.8 6.5 %copy.20 = bf16[48,168,128]{0,2,1:T(8,128)(2,1)} copy(bf16[48,168,128]{2,1,0:T(8,128)(2,1)} %shard_map.37) | data formatting | bytes 4128768 | tf_op jit(solution)/shard_map/pallas_call | solution.py:70
  76.3 11.3 %copy.21 = bf16[4,2,2,48,84,16]{3,2,1,5,4,0:T(2,128)(2,1)} copy(bf16[4,2,2,48,84,16]{3,5,0,1,2,4:T(8,128)(2,1)} %bitcast.35) | data formatting | bytes 4128768 | tf_op jit(solution)/shard_map/transpose | solution.py:135
  87.6 10.3 %reshape.208 = bf16[4,192,1344]{1,2,0:T(8,128)(2,1)S(1)} reshape(bf16[4,2,2,48,84,16]{3,2,1,5,4,0:T(2,128)(2,1)} %copy.21) | data formatting | bytes 4128768 | tf_op jit(solution)/shard_map/reshape | solution.py:138
  97.9 2.5 %copy.22 = bf16[4,192,1344]{2,1,0:T(8,128)(2,1)} copy(bf16[4,192,1344]{1,2,0:T(8,128)(2,1)S(1)} %reshape.208) | data formatting | bytes 4128768 | tf_op jit(solution)/shard_map/reshape | solution.py:138
  100.5 5.2 %all-to-all-start = ((bf16[4,192,1344]{2,1,0:T(8,128)(2,1)}), bf16[4,192,1344]{2,1,0:T(8,128)(2,1)S(1)}, u32[]{:S(2)}, u32[]{:S(2)}) async-start(bf16[4,192,1344]{2,1,0:T(8,128)(2,1)} %copy.22), calls=%async_computation | async-start | bytes 4325376 | tf_op jit(solution)/shard_map/all_to_all | solution.py:139
  105.7 0.1 fusion.8
  105.8 25.5 %all-to-all-done = bf16[4,192,1344]{2,1,0:T(8,128)(2,1)S(1)} async-done(((bf16[4,192,1344]{2,1,0:T(8,128)(2,1)}), bf16[4,192,1344]{2,1,0:T(8,128)(2,1)S(1)}, u32[]{:S(2)}, u32[]{:S(2)}) %all-to-all-start) | async-done | bytes 2064416 | tf_op jit(solution)/shard_map/all_to_all | solution.py:139
  131.3 1.3 copy-done
  132.6 0.1 broadcast_add_fusion
  132.7 10.7 %multiply_convert_fusion.1 = (bf16[4,2,1,48,1440]{4,3,2,1,0:T(8,128)(2,1)S(1)}, bf16[4,2,1,48,1440]{4,3,2,1,0:T(8,128)(2,1)S(1)}) fusion(s32[4,2,48]{2,1,0:T(2,128)S(1)} %broadcast_add_fusion, f32[4,2,48]{2,1,0:T(2,128)S(1)} %fusion.8), kind=kLoop, calls=%fused_computation.10 | loop fusion | flops 7188480 | bytes 2214912 | tf_op jit(solution)/shard_map/convert
  143.4 1.6 pad_maximum_fusion
  145.0 53.6 %all-reduce.5.cloned.1.call-done = bf16[768,1344]{1,0:T(8,128)(2,1)} async-done(((bf16[768,1344]{1,0:T(8,128)(2,1)}), bf16[768,1344]{1,0:T(8,128)(2,1)}) %all-reduce.5.cloned.1.call-update) | async-done | bytes 2064400 | tf_op jit(solution)/shard_map/psum | solution.py:158
  198.6 3.6 %fusion.7 = bf16[1344,768]{0,1:T(8,128)(2,1)} fusion(bf16[768,1344]{1,0:T(8,128)(2,1)} %all-reduce.5.cloned.1.call-done, bf16[4,192,1344]{2,1,0:T(8,128)(2,1)S(1)} %copy-done.1), kind=kLoop, calls=%fused_computation.15 | loop fusion | flops 5160960 | bytes 6193152 | tf_op jit(solution)/shard_map/dot_general | solution.py:161
  202.3 4.3 %copy.23 = bf16[1344,768]{1,0:T(8,128)(2,1)} copy(bf16[1344,768]{0,1:T(8,128)(2,1)} %fusion.7) | data formatting | bytes 4128768 | tf_op jit(solution)/shard_map/dot_general | solution.py:161
  206.5 7.2 %fusion.1 = bf16[1,84,16,1440]{3,2,1,0:T(8,128)(2,1)} fusion(bf16[1,84,16,1440]{3,2,1,0:T(8,128)(2,1)} %param.3, bf16[84,16,768]{2,1,0:T(8,128)(2,1)} %bitcast.38, bf16[768,1440,1]{1,0,2:T(8,128)(2,1)S(1)} %bitcast.37, f32[84]{0:T(128)S(1)} %copy-done.3), kind=kOutput, calls=%fused_computation.3 | convolution fusion | flops 2980454400 | bytes 12018000 | tf_op jit(solution)/shard_map/dot_general | solution.py:161
  (23 shorter events, 0.4 us)
Async XLA Ops:
  100.5 30.8 %all-to-all-start = ((bf16[4,192,1344]{2,1,0:T(8,128)(2,1)}), bf16[4,192,1344]{2,1,0:T(8,128)(2,1)S(1)}, u32[]{:S(2)}, u32[]{:S(2)}) async-start(bf16[4,192,1344]{2,1,0:T(8,128)(2,1)} %copy.22), calls=%async_computation | async-start | bytes 4325376 | tf_op jit(solution)/shard_map/all_to_all | solution.py:139
  105.7 93.0 %all-reduce.5.cloned.1.call-start = ((), (), s32[]{:S(2)}) async-start(), calls=%async_computation.1 | async-start | bytes 4325376 | tf_op jit(solution)/shard_map/psum | solution.py:158
  131.2 1.3 copy-start
  143.4 55.2 %copy-start.1 = (bf16[4,192,1344]{2,1,0:T(8,128)(2,1)S(1)}, bf16[4,192,1344]{2,1,0:T(8,128)(2,1)}, u32[]{:S(2)}) copy-start(bf16[4,192,1344]{2,1,0:T(8,128)(2,1)} %copy-done) | copy-start | bytes 6193156
  202.2 4.3 %copy-start.2 = (bf16[4,2,2,48,1440]{4,3,2,1,0:T(8,128)(2,1)S(1)}, bf16[4,2,2,48,1440]{4,3,2,1,0:T(8,128)(2,1)}, u32[]{:S(2)}) copy-start(bf16[4,2,2,48,1440]{4,3,2,1,0:T(8,128)(2,1)} %pad_maximum_fusion) | copy-start | bytes 6635524
  202.2 4.3 %copy-start.3 = (f32[84]{0:T(128)S(1)}, f32[84]{0:T(128)}, u32[]{:S(2)}) copy-start(f32[84]{0:T(128)} %param.5) | copy-start | bytes 1012
Sparse Core Ops, SparseCore 0:
  132.7 65.8 all-reduce.4

commit v2 on v1

--- a/solution.py
+++ b/solution.py
@@ -19,7 +19,53 @@
     return jnp.concatenate([jnp.zeros((1,), jnp.float32), jnp.cumsum(terms)])
 
 
-def synthesis_kernel(block, pitch, order_ref, cosine_ref, diagonal_ref, spectral_ref, out_ref, table):
+def spectral_kernel(order_local, degree_count, pitch, coef_ref, out_ref, turned):
+    rows, padded, degrees = coef_ref.shape
+    first = lax.axis_index("space") * order_local
+    factor = math.sqrt(3.0) * math.sqrt(4.0 * math.pi) / degree_count * 2.0 ** (-30)
+    tiles = degrees // 128
+    keeps = []
+    for tile in range(tiles):
+        slot = lax.broadcasted_iota(jnp.int32, (padded, 128), 0)
+        degree = lax.broadcasted_iota(jnp.int32, (padded, 128), 1) + tile * 128
+        keeps.append((degree >= slot + first) & (degree < degree_count) & (slot < order_local))
+
+    def convert(row, carry):
+        for tile in range(tiles):
+            values = coef_ref[row, :, tile * 128 : tile * 128 + 128].astype(jnp.float32) * factor
+            start = pl.multiple_of((tile * rows + row) * pitch, 8)
+            turned[pl.ds(start, padded), :] = jnp.where(keeps[tile], values, 0.0)
+        return carry
+
+    lax.fori_loop(0, rows, convert, 0)
+
+    def collect(slot, carry):
+        for tile in range(tiles):
+            values = turned[pl.ds(tile * rows * pitch + slot, rows, stride=pitch), :]
+            out_ref[slot, :, tile * 128 : tile * 128 + 128] = values.astype(jnp.bfloat16)
+        return carry
+
+    lax.fori_loop(0, padded, collect, 0, unroll=8)
+
+
+def turn_spectral(coefficients, padded, degrees, degree_count):
+    rows, order_local, _ = coefficients.shape
+    block = 24 if rows % 24 == 0 else 8
+    pitch = padded + 8
+    return pl.pallas_call(
+        functools.partial(spectral_kernel, order_local, degree_count, pitch),
+        grid=(rows // block,),
+        out_shape=jax.ShapeDtypeStruct((padded, rows, degrees), jnp.bfloat16),
+        in_specs=[pl.BlockSpec((block, padded, degrees), lambda i: (i, 0, 0))],
+        out_specs=pl.BlockSpec((padded, block, degrees), lambda i: (0, i, 0)),
+        scratch_shapes=[pltpu.VMEM((degrees // 128 * block * pitch, 128), jnp.float32)],
+        compiler_params=pltpu.CompilerParams(vmem_limit_bytes=48 * 1024 * 1024),
+    )(coefficients)
+
+
+def synthesis_kernel(
+    block, pitch, lat, order_ref, cosine_ref, diagonal_ref, spectral_ref, out_ref, table, kept
+):
     half, lanes = order_ref.shape
     degrees = spectral_ref.shape[-1]
 
@@ -51,6 +97,11 @@
     first = pl.program_id(0) * block
     rows = spectral_ref.shape[2]
     low = lax.broadcasted_iota(jnp.int32, (rows, lanes), 1) < lanes // 2
+    pack = 128 // lat
+    bands = lanes // 2 // lat
+    groups = out_ref.shape[-1] // 128
+    kept_rows = groups * pack * 2
+    deep = half + 8
     for inner in range(block):
         tiles = []
         for tile in range(lanes // 128):
@@ -59,28 +110,256 @@
         values = jnp.concatenate(tiles, axis=1)
         both = jnp.concatenate([spectral_ref[0, inner], spectral_ref[1, inner]], axis=0)
         found = jnp.dot(both, values, preferred_element_type=jnp.float32)
-        out_ref[inner] = jnp.where(low, found[:rows], found[rows:]).astype(jnp.bfloat16)
-
-
-def synthesize(spectral, order_plane, cosine_row, diagonal_plane):
+        found = jnp.where(low, found[:rows], found[rows:])
+        for tile in range(lanes // 128):
+            kept[pl.ds(tile * kept_rows * deep + first + inner, rows, stride=deep), :] = found[
+                :, tile * 128 : tile * 128 + 128
+            ]
+
+    @pl.when(pl.program_id(0) == pl.num_programs(0) - 1)
+    def regroup():
+        chunk = lax.broadcasted_iota(jnp.int32, (half, 128), 1) // lat
+        for tile in range(lanes // 128):
+            for spare in range(rows, kept_rows):
+                kept[pl.ds((tile * kept_rows + spare) * deep, half), :] = order_ref[:, :128] * 0.0
+
+            def one_group(group, carry):
+                for part in range(2):
+                    planes = []
+                    for spot in range(pack):
+                        row = tile * kept_rows + (group * pack + spot) * 2 + part
+                        planes.append(kept[pl.ds(pl.multiple_of(row * deep, 8), half), :])
+                    gap = 1
+                    while gap < pack:
+                        upper = (chunk // gap) % 2 == 1
+                        for spot in range(pack):
+                            if (spot // gap) % 2 == 0:
+                                one, two = planes[spot], planes[spot + gap]
+                                planes[spot] = jnp.where(upper, pltpu.roll(two, gap * lat, 1), one)
+                                planes[spot + gap] = jnp.where(
+                                    upper, two, pltpu.roll(one, 128 - gap * lat, 1)
+                                )
+                        gap *= 2
+                    for spot in range(pack):
+                        high, band = divmod(tile * pack + spot, bands)
+                        lane = pl.multiple_of(group * 128, 128)
+                        out_ref[band, high, part, :, pl.ds(lane, 128)] = planes[spot].astype(
+                            jnp.bfloat16
+                        )
+                return carry
+
+            lax.fori_loop(0, groups, one_group, 0)
+
+
+def synthesize(spectral, order_plane, cosine_row, diagonal_plane, lat):
     pair, half, rows, degrees = spectral.shape
     lanes = order_plane.shape[1]
     block = 8
     pitch = degrees + 8
+    pack = 128 // lat
+    groups = round_up(rows // 2, pack) // pack
+    out_dims = (lanes // 2 // lat, 2, 2, half, groups * 128)
+    kept_rows = lanes // 128 * groups * pack * 2 * (half + 8)
     return pl.pallas_call(
-        functools.partial(synthesis_kernel, block, pitch),
+        functools.partial(synthesis_kernel, block, pitch, lat),
         grid=(half // block,),
-        out_shape=jax.ShapeDtypeStruct((half, rows, lanes), jnp.bfloat16),
+        out_shape=jax.ShapeDtypeStruct(out_dims, jnp.bfloat16),
         in_specs=[
             pl.BlockSpec((half, lanes), lambda i: (0, 0)),
             pl.BlockSpec((1, lanes), lambda i: (0, 0)),
             pl.BlockSpec((half, lanes), lambda i: (0, 0)),
             pl.BlockSpec((pair, block, rows, degrees), lambda i: (0, i, 0, 0)),
         ],
-        out_specs=pl.BlockSpec((block, rows, lanes), lambda i: (i, 0, 0)),
-        scratch_shapes=[pltpu.VMEM((lanes // 128 * half * pitch, 128), jnp.float32)],
+        out_specs=pl.BlockSpec(out_dims, lambda i: (0, 0, 0, 0, 0)),
+        scratch_shapes=[
+            pltpu.VMEM((lanes // 128 * half * pitch, 128), jnp.float32),
+            pltpu.VMEM((kept_rows, 128), jnp.float32),
+        ],
         compiler_params=pltpu.CompilerParams(vmem_limit_bytes=60 * 1024 * 1024),
     )(order_plane, cosine_row, diagonal_plane, spectral)
+
+
+def exchange_kernel(parts, sent, out, raw, near, sums, lower, other, total, *sems):
+    a2a_send, a2a_recv = sems[0], sems[1]
+    pair = {
+        "near": (sems[2], sems[3]),
+        "line": (sems[4], sems[5]),
+        "swap": (sems[6], sems[7]),
+        "back": (sems[8], sems[9]),
+        "mate": (sems[10], sems[11]),
+    }
+    bands, depth, _ = sent.shape
+    member_count = lax.axis_size("member")
+    chips = member_count // 2
+    middle = chips // 2
+    me = lax.axis_index("member")
+    space = lax.axis_index("space")
+    core = lax.rem(me, 2)
+    chip = me // 2
+    mate = chip * 2 + 1 - core
+    left = chip < middle
+    rank = jnp.where(left, chip, chips - 1 - chip)
+    inward = jnp.where(left, chip + 1, chip - 1) * 2 + core
+    outward = jnp.where(left, chip - 1, chip + 1) * 2 + core
+    step = depth // (2 * parts)
+    mesh_ids = pl.DeviceIdType.MESH
+
+    def spread(k, hop):
+        rows = pl.ds(k * 2 * step, 2 * step)
+        target = lax.rem(space + hop, bands)
+        return pltpu.make_async_remote_copy(
+            src_ref=sent.at[target, rows],
+            dst_ref=raw.at[space, rows],
+            send_sem=a2a_send.at[k, hop],
+            recv_sem=a2a_recv.at[k, hop],
+            device_id={"space": target},
+            device_id_type=mesh_ids,
+        )
+
+    def hand(kind, k, source, landing, target):
+        return pltpu.make_async_remote_copy(
+            src_ref=source,
+            dst_ref=landing,
+            send_sem=pair[kind][0].at[k],
+            recv_sem=pair[kind][1].at[k],
+            device_id={"member": target},
+            device_id_type=mesh_ids,
+        )
+
+    def half_rows(k, which):
+        return pl.ds(pl.multiple_of((k * 2 + which) * step, step), step)
+
+    def near_copy(k):
+        return hand("near", k, raw.at[:, half_rows(k, 1 - core)], near.at[k], mate)
+
+    def line_copy(k):
+        return hand("line", k, sums.at[k], lower.at[k], inward)
+
+    def swap_copy(k):
+        return hand("swap", k, sums.at[k], other.at[k], inward)
+
+    def back_copy(k):
+        return hand("back", k, total.at[k, core], total.at[k, core], outward)
+
+    def mate_copy(k):
+        return hand("mate", k, total.at[k, core], total.at[k, core], mate)
+
+    def stage_near(k):
+        for hop in range(1, bands):
+            spread(k, hop).wait_recv()
+        near_copy(k).start()
+
+    def send_inward(k, level):
+        @pl.when(rank == level)
+        def _():
+            if level == middle - 1:
+                swap_copy(k).start()
+            else:
+                line_copy(k).start()
+
+    def stage_sum(k):
+        near_copy(k).wait_recv()
+        mine = raw[:, half_rows(k, core)].astype(jnp.float32) + near[k].astype(jnp.float32)
+        sums[k] = mine.astype(jnp.bfloat16)
+        send_inward(k, 0)
+
+    def stage_line(level, k):
+        @pl.when(rank == level)
+        def _():
+            line_copy(k).wait_recv()
+            both = sums[k].astype(jnp.float32) + lower[k].astype(jnp.float32)
+            sums[k] = both.astype(jnp.bfloat16)
+
+        send_inward(k, level)
+
+    def send_outward(k, level):
+        if level > 0:
+            back_copy(k).start()
+        mate_copy(k).start()
+
+    def stage_swap(k):
+        @pl.when(rank == middle - 1)
+        def _():
+            swap_copy(k).wait_recv()
+            both = sums[k].astype(jnp.float32) + other[k].astype(jnp.float32)
+            total[k, core] = both.astype(jnp.bfloat16)
+            send_outward(k, middle - 1)
+
+    def stage_back(level, k):
+        @pl.when(rank == level)
+        def _():
+            back_copy(k).wait_recv()
+            send_outward(k, level)
+
+    def stage_out(k):
+        mate_copy(k).wait_recv()
+        for which in range(2):
+            rows = pl.ds((k * 2 + which) * step, step)
+            mean = total[k, which].astype(jnp.float32) * (1.0 / member_count)
+            out[:, rows] = (raw[:, rows].astype(jnp.float32) - mean).astype(jnp.bfloat16)
+
+    stages = [stage_near, stage_sum]
+    stages += [functools.partial(stage_line, level) for level in range(1, middle)]
+    stages += [stage_swap]
+    stages += [functools.partial(stage_back, level) for level in range(middle - 2, -1, -1)]
+    stages += [stage_out]
+
+    for k in range(parts):
+        for hop in range(1, bands):
+            spread(k, hop).start()
+    raw[space] = sent[space]
+    for turn in range(parts + len(stages) - 1):
+        for place in reversed(range(len(stages))):
+            k = turn - place
+            if 0 <= k < parts:
+                stages[place](k)
+
+    for k in range(parts):
+        for hop in range(1, bands):
+            spread(k, hop).wait_send()
+        near_copy(k).wait_send()
+        mate_copy(k).wait_send()
+
+        @pl.when(rank == middle - 1)
+        def _():
+            swap_copy(k).wait_send()
+
+        @pl.when(rank < middle - 1)
+        def _():
+            line_copy(k).wait_send()
+
+        @pl.when(rank > 0)
+        def _():
+            back_copy(k).wait_send()
+
+
+def exchange(found):
+    bands, depth, width = found.shape
+    parts = next(p for p in (6, 3, 2, 1) if depth % (32 * p) == 0)
+    step = depth // (2 * parts)
+    buffer = pltpu.VMEM((parts, bands, step, width), jnp.bfloat16)
+    dma = pltpu.SemaphoreType.DMA
+    vmem = pl.BlockSpec(memory_space=pltpu.VMEM)
+    return pl.pallas_call(
+        functools.partial(exchange_kernel, parts),
+        out_shape=jax.ShapeDtypeStruct(found.shape, jnp.bfloat16),
+        in_specs=[vmem],
+        out_specs=vmem,
+        scratch_shapes=[
+            pltpu.VMEM((bands, depth, width), jnp.bfloat16),
+            buffer,
+            buffer,
+            buffer,
+            buffer,
+            pltpu.VMEM((parts, 2, bands, step, width), jnp.bfloat16),
+            dma((parts, bands)),
+            dma((parts, bands)),
+        ]
+        + [dma((parts,))] * 10,
+        compiler_params=pltpu.CompilerParams(
+            has_side_effects=True, vmem_limit_bytes=56 * 1024 * 1024
+        ),
+    )(found)
 
 
 def local(weather, coefficients, channel_scale):
@@ -121,22 +400,14 @@
     order_plane = pair_up(jnp.broadcast_to(order_values, (padded, lat_count)))
     cosine_row = jnp.tile(jnp.cos(colatitude), 2)[None, :]
 
-    degrees = jnp.arange(degree_count, dtype=jnp.int32)
-    keep = degrees[None, :] >= orders[:order_local, None]
-    factor = math.sqrt(3.0) * math.sqrt(4.0 * math.pi) / degree_count * 2.0 ** (-30)
-    spectral = jnp.where(keep, coefficients.astype(jnp.float32) * factor, 0.0).astype(jnp.bfloat16)
-    spectral = spectral.transpose(3, 0, 1, 2, 4).reshape(order_local, rows, degree_count)
-    spectral = jnp.pad(
-        spectral, ((0, padded - order_local), (0, 0), (0, degrees_padded - degree_count))
+    spectral = turn_spectral(
+        coefficients.reshape(rows, order_local, degree_count), padded, degrees_padded, degree_count
     ).reshape(2, half, rows, degrees_padded)
-    found = synthesize(spectral, order_plane, cosine_row, pair_up(diagonal))
-
-    found = found.reshape(half, member_local * channels, 2, 2, band_count, rows_local)
-    found = found.transpose(4, 3, 2, 0, 1, 5)
+    found = synthesize(spectral, order_plane, cosine_row, pair_up(diagonal), rows_local)
     depth = padded * 2
     flat = member_local * channels * rows_local
-    found = found.reshape(band_count, depth, flat)
-    own = lax.all_to_all(found, "space", split_axis=0, concat_axis=0, tiled=True)
+    found = found.reshape(band_count, depth, -1)
+    centred = exchange(found)
 
     band = jnp.arange(band_count, dtype=jnp.int32)[:, None]
     slot = slots.reshape(2, half)
@@ -153,11 +424,7 @@
     ).astype(jnp.bfloat16)
     basis = basis.reshape(band_count * depth, lon_count)
 
-    own = own.reshape(band_count * depth, flat)
-    split = own.astype(jnp.float32).reshape(band_count * depth, member_local, -1)
-    total = lax.psum(jnp.sum(split, axis=1).astype(jnp.bfloat16), "member").astype(jnp.float32)
-    centred = (split - total[:, None, :] * (1.0 / member_count)).astype(jnp.bfloat16)
-    centred = centred.reshape(band_count * depth, flat)
+    centred = centred.reshape(band_count * depth, -1)[:, :flat]
     noise = lax.dot_general(
         centred, basis, (((0,), (0,)), ((), ())), preferred_element_type=jnp.float32
     )

time: 221 us -> 144 us (0.65)
  Pallas kernels: 15.3 us -> 101 us
  waiting for transfers between devices: 79.1 us -> 0 us
  local copies, waits for them, and re-layouts: 65.1 us -> 25 us
  other arithmetic: 35.1 us -> 12.6 us
  between operations: 13.5 us -> 0.1 us
  starting transfers between devices: 5.2 us -> 0 us
    pallas_call x1 -> x3, Pallas kernels: 15.3 us -> 101 us  [the longest x1 63.2 us: exchange(): pl.pallas_call(functools.partial(exchange_kernel, parts), out_shape=jax.S...]
    psum x1 -> x0, waiting for transfers between devices: 53.6 us -> none  [local(): lax.psum(jnp.sum(split, axis=1).astype(jnp.bfloat16), 'member')]
    all_to_all x1 -> x0, waiting for transfers between devices: 25.5 us -> none  [local(): lax.all_to_all(found, 'space', split_axis=0, concat_axis=0, tiled=True)]
    transpose x1 -> x0, other arithmetic: 16.8 us -> none  [local(): spectral.transpose(3, 0, 1, 2, 4).reshape(order_local, rows, degree_count)]
    transpose x2 -> x0, local copies, waits for them, and re-layouts: 13.5 us -> none  [the longest x1 11.3 us: local(): found = found.transpose(4, 3, 2, 0, 1, 5)]
    reshape x3 -> x1, local copies, waits for them, and re-layouts: 12.9 us -> 0.01 us  [the longest x2 12.9 us: local(): found = found.reshape(band_count, depth, flat)]
    pad x1 -> x0, local copies, waits for them, and re-layouts: 10.6 us -> none  [local(): jnp.pad(spectral, ((0, padded - order_local), (0, 0), (0, degrees_padded...]
    pallas_call x1 -> x0, local copies, waits for them, and re-layouts: 6.5 us -> none  [synthesize(): pl.pallas_call(functools.partial(synthesis_kernel, block, pitch), grid=(h...]
  transfers between devices with their start and end apart: 2 -> 0, of which waited for: 2 -> 0; matrix products, arithmetic and copies ran while one was open for 6% -> 0% of each run, Pallas kernels for 0% -> 0%
where the time goes in v2:
time: 144 us
  Pallas kernels  101 us (70%)
  local copies, waits for them, and re-layouts  25 us (17%)
  other arithmetic  12.6 us (9%)
  matrix products  5.09 us (4%)
    pallas_call x1, Pallas kernels, exchange(): pl.pallas_call(functools.partial(exchange_kernel, parts), out_shape=jax.S...  63.2 us
    unnamed x7, local copies, waits for them, and re-layouts  19.7 us
    pallas_call x1, Pallas kernels, synthesize(): pl.pallas_call(functools.partial(synthesis_kernel, block, pitch, lat), gr...  19.4 us
    pallas_call x1, Pallas kernels, turn_spectral(): pl.pallas_call(functools.partial(spectral_kernel, order_local, degree_cou...  18.5 us
    another operation x4, other arithmetic  11.1 us
    dot_general x1, matrix products, local(): lax.dot_general(centred, basis, (((0,), (0,)), ((), ())), preferred_eleme...  5.09 us
    dot_general x2, local copies, waits for them, and re-layouts, local(): lax.dot_general(centred, basis, (((0,), (0,)), ((), ())), preferred_eleme...  4.11 us

profile of v2, /device:TPU:0, one launch (start us, length us, event | category | flops | bytes accessed | tf_op | source)
XLA Modules:
  0.0 143.8 jit_solution(690839256025818991)
XLA Ops:
  0.0 0.3 reduce-window.9
  0.3 0.1 slice.37
  0.4 0.1 slice_reduce_fusion
  0.6 0.1 add_bitcast_fusion
  0.6 0.1 select_maximum_fusion
  0.7 0.1 dynamic-slice_add_fusion
  0.9 0.1 add_exponential_fusion
  1.0 0.1 slice_bitcast_fusion.2
  1.1 0.1 broadcast_in_dim.38
  1.1 0.1 broadcast_in_dim.39
  1.2 0.7 pad_maximum_fusion.1
  1.9 18.4 %copy.6 = s32[1,84,2,91,361]{4,3,2,1,0:T(8,128)} copy(s32[1,84,2,91,361]{4,2,3,1,0:T(2,128)} %param.4) | data formatting | bytes 44151744 | tf_op args[1]
  20.3 18.5 %shard_map.37 = bf16[96,168,384]{2,1,0:T(8,128)(2,1)} custom-call(s32[168,91,361]{2,1,0:T(8,128)} %bitcast.25), custom_call_target="tpu_custom_call" | custom-call | tf_op jit(solution)/shard_map/pallas_call | solution.py:55
  38.8 0.7 broadcast_in_dim_tile.3.cosine_ref
  39.5 19.4 %shard_map.38 = bf16[4,2,2,48,1408]{4,3,2,1,0:T(8,128)(2,1)} custom-call(f32[48,128]{1,0:T(8,128)} %get-tuple-element.11.order_ref, f32[1,128]{1,0:T(1,128)} %broadcast_in_dim_tile.3.cosine_ref, f32[48,128]{1,0:T(8,128)} %get-tuple-element.12.diagonal_ref, bf16[2,48,168,384]{3,2,1,0:T(8,128)(2,1)} %bitcast.26), custom_call_target="tpu_custom_call" | custom-call | tf_op jit(solution)/shard_map/pallas_call | solution.py:163
  58.9 63.2 %shard_map.39 = bf16[4,192,1408]{2,1,0:T(8,128)(2,1)} custom-call(bf16[4,192,1408]{2,1,0:T(8,128)(2,1)} %bitcast.27), custom_call_target="tpu_custom_call" | custom-call | tf_op jit(solution)/shard_map/pallas_call | solution.py:343
  122.1 1.8 %slice_bitcast_fusion = bf16[1344,768]{0,1:T(8,128)(2,1)S(1)} fusion(bf16[768,1408]{1,0:T(8,128)(2,1)} %bitcast.28), kind=kLoop, calls=%fused_computation.12 | loop fusion | bytes 4128768 | tf_op jit(solution)/shard_map/dot_general | solution.py:428
  123.9 2.3 %copy.7 = bf16[1344,768]{1,0:T(8,128)(2,1)} copy(bf16[1344,768]{0,1:T(8,128)(2,1)S(1)} %slice_bitcast_fusion) | data formatting | bytes 4128768 | tf_op jit(solution)/shard_map/dot_general | solution.py:428
  126.3 0.1 fusion.6
  126.3 0.1 broadcast_add_fusion
  126.4 0.0 copy-start.1
  126.4 10.7 %multiply_convert_fusion.1 = (bf16[4,2,1,48,1440]{4,3,2,1,0:T(8,128)(2,1)S(1)}, bf16[4,2,1,48,1440]{4,3,2,1,0:T(8,128)(2,1)S(1)}) fusion(s32[4,2,48]{2,1,0:T(2,128)S(1)} %broadcast_add_fusion, f32[4,2,48]{2,1,0:T(2,128)S(1)} %fusion.6), kind=kLoop, calls=%fused_computation.7 | loop fusion | flops 7188480 | bytes 2214912 | tf_op jit(solution)/shard_map/convert
  137.1 0.0 copy-start
  137.1 0.0 copy-start.2
  137.1 0.2 pad_maximum_fusion
  137.4 0.0 copy-done.1
  137.4 1.3 copy-done
  138.7 0.0 copy-done.2
  138.7 5.1 %fusion = bf16[1,84,16,1440]{3,2,1,0:T(8,128)(2,1)} fusion(bf16[1,84,16,1440]{3,2,1,0:T(8,128)(2,1)S(1)} %copy-done.1, bf16[84,16,768]{2,1,0:T(8,128)(2,1)S(1)} %bitcast.30, bf16[768,1440,1]{1,0,2:T(8,128)(2,1)S(1)} %bitcast.29, f32[84]{0:T(128)S(1)} %copy-done.2), kind=kOutput, calls=%fused_computation.1 | convolution fusion | flops 2980454400 | bytes 12018000 | tf_op jit(solution)/shard_map/dot_general | solution.py:428
  (12 shorter events, 0.2 us)
Async XLA Ops:
  126.4 11.0 %copy-start.1 = (bf16[1,84,16,1440]{3,2,1,0:T(8,128)(2,1)S(1)}, bf16[1,84,16,1440]{3,2,1,0:T(8,128)(2,1)}, u32[]{:S(2)}) copy-start(bf16[1,84,16,1440]{3,2,1,0:T(8,128)(2,1)} %param.3) | copy-start | bytes 11612164
  137.1 1.6 %copy-start = (bf16[1344,768]{1,0:T(8,128)(2,1)S(1)}, bf16[1344,768]{1,0:T(8,128)(2,1)}, u32[]{:S(2)}) copy-start(bf16[1344,768]{1,0:T(8,128)(2,1)} %copy.7) | copy-start | bytes 6193156
  137.1 1.6 %copy-start.2 = (f32[84]{0:T(128)S(1)}, f32[84]{0:T(128)}, u32[]{:S(2)}) copy-start(f32[84]{0:T(128)} %param.5) | copy-start | bytes 1012

commit v3 on v2

--- a/solution.py
+++ b/solution.py
@@ -19,55 +19,42 @@
     return jnp.concatenate([jnp.zeros((1,), jnp.float32), jnp.cumsum(terms)])
 
 
-def spectral_kernel(order_local, degree_count, pitch, coef_ref, out_ref, turned):
-    rows, padded, degrees = coef_ref.shape
-    first = lax.axis_index("space") * order_local
-    factor = math.sqrt(3.0) * math.sqrt(4.0 * math.pi) / degree_count * 2.0 ** (-30)
-    tiles = degrees // 128
-    keeps = []
-    for tile in range(tiles):
-        slot = lax.broadcasted_iota(jnp.int32, (padded, 128), 0)
-        degree = lax.broadcasted_iota(jnp.int32, (padded, 128), 1) + tile * 128
-        keeps.append((degree >= slot + first) & (degree < degree_count) & (slot < order_local))
-
-    def convert(row, carry):
-        for tile in range(tiles):
-            values = coef_ref[row, :, tile * 128 : tile * 128 + 128].astype(jnp.float32) * factor
-            start = pl.multiple_of((tile * rows + row) * pitch, 8)
-            turned[pl.ds(start, padded), :] = jnp.where(keeps[tile], values, 0.0)
-        return carry
-
-    lax.fori_loop(0, rows, convert, 0)
-
-    def collect(slot, carry):
-        for tile in range(tiles):
-            values = turned[pl.ds(tile * rows * pitch + slot, rows, stride=pitch), :]
-            out_ref[slot, :, tile * 128 : tile * 128 + 128] = values.astype(jnp.bfloat16)
-        return carry
-
-    lax.fori_loop(0, padded, collect, 0, unroll=8)
-
-
-def turn_spectral(coefficients, padded, degrees, degree_count):
-    rows, order_local, _ = coefficients.shape
-    block = 24 if rows % 24 == 0 else 8
-    pitch = padded + 8
-    return pl.pallas_call(
-        functools.partial(spectral_kernel, order_local, degree_count, pitch),
-        grid=(rows // block,),
-        out_shape=jax.ShapeDtypeStruct((padded, rows, degrees), jnp.bfloat16),
-        in_specs=[pl.BlockSpec((block, padded, degrees), lambda i: (i, 0, 0))],
-        out_specs=pl.BlockSpec((padded, block, degrees), lambda i: (0, i, 0)),
-        scratch_shapes=[pltpu.VMEM((degrees // 128 * block * pitch, 128), jnp.float32)],
-        compiler_params=pltpu.CompilerParams(vmem_limit_bytes=48 * 1024 * 1024),
-    )(coefficients)
-
-
 def synthesis_kernel(
-    block, pitch, lat, order_ref, cosine_ref, diagonal_ref, spectral_ref, out_ref, table, kept
+    block, lat, order_ref, cosine_ref, diagonal_ref, coef, tail, out_ref, table, kept, held, arrived
 ):
     half, lanes = order_ref.shape
-    degrees = spectral_ref.shape[-1]
+    channels, order_local, _, degree_count = coef.shape
+    rows, tiles = held.shape[1], held.shape[2]
+    degrees = tiles * 128
+    pitch = degrees + 8
+    factor = math.sqrt(3.0) * math.sqrt(4.0 * math.pi) / degree_count * 2.0 ** (-30)
+    turn = pl.program_id(0)
+    flat = held.reshape(held.shape[0] * rows * tiles * 2, 128)
+
+    def fetch(step, act):
+        base = lax.rem(step, 2) * (2 * block)
+        for spot in range(2 * block):
+            slot = step * block + spot % block + spot // block * half
+            slot = jnp.minimum(slot, order_local - 1)
+            for tile in range(tiles):
+                if tile < tiles - 1:
+                    source = coef.at[:, slot, :, pl.ds(tile * 128, 128)]
+                else:
+                    source = tail.at[:, slot]
+                copy = pltpu.make_async_copy(
+                    source,
+                    held.at[base + spot, pl.ds(0, channels), tile],
+                    arrived.at[base + spot, tile],
+                )
+                act(copy)
+
+    @pl.when(turn == 0)
+    def begin():
+        fetch(turn, lambda copy: copy.start())
+
+    @pl.when(turn + 1 < pl.num_programs(0))
+    def ahead():
+        fetch(turn + 1, lambda copy: copy.start())
 
     @pl.when(pl.program_id(0) == 0)
     def build():
@@ -94,40 +81,57 @@
         zero = order * 0.0
         lax.fori_loop(0, degrees, advance, (zero, zero, zero), unroll=4)
 
-    first = pl.program_id(0) * block
-    rows = spectral_ref.shape[2]
+    fetch(turn, lambda copy: copy.wait())
+    first = turn * block
     low = lax.broadcasted_iota(jnp.int32, (rows, lanes), 1) < lanes // 2
     pack = 128 // lat
     bands = lanes // 2 // lat
     groups = out_ref.shape[-1] // 128
-    kept_rows = groups * pack * 2
     deep = half + 8
+    lane = lax.broadcasted_iota(jnp.int32, (rows, 128), 1)
+    first_order = lax.axis_index("space") * order_local
+
+    def read(spot, slot, part):
+        base = (lax.rem(turn, 2) * (2 * block) + spot) * (rows * tiles * 2)
+        pieces = []
+        for tile in range(tiles):
+            values = flat[pl.ds(base + tile * 2 + part, rows, stride=tiles * 2), :]
+            degree = lane + tile * 128
+            least = jnp.where(slot < order_local, first_order + slot, degrees)
+            keep = (degree >= least) & (degree < degree_count)
+            pieces.append(jnp.where(keep, values.astype(jnp.float32) * factor, 0.0))
+        return jnp.concatenate(pieces, axis=1)
+
     for inner in range(block):
-        tiles = []
+        columns = []
         for tile in range(lanes // 128):
             start = pl.multiple_of((tile * half + first + inner) * pitch, 8)
-            tiles.append(table[pl.ds(start, degrees), :].astype(jnp.bfloat16))
-        values = jnp.concatenate(tiles, axis=1)
-        both = jnp.concatenate([spectral_ref[0, inner], spectral_ref[1, inner]], axis=0)
-        found = jnp.dot(both, values, preferred_element_type=jnp.float32)
-        found = jnp.where(low, found[:rows], found[rows:])
-        for tile in range(lanes // 128):
-            kept[pl.ds(tile * kept_rows * deep + first + inner, rows, stride=deep), :] = found[
-                :, tile * 128 : tile * 128 + 128
-            ]
+            columns.append(table[pl.ds(start, degrees), :].astype(jnp.bfloat16))
+        values = jnp.concatenate(columns, axis=1)
+        stacked = [
+            read(inner + side * block, first + inner + side * half, part)
+            for side in range(2)
+            for part in range(2)
+        ]
+        stacked = jnp.concatenate(stacked, axis=0).astype(jnp.bfloat16)
+        found = jnp.dot(stacked, values, preferred_element_type=jnp.float32)
+        for part in range(2):
+            one = found[part * rows : part * rows + rows]
+            two = found[(2 + part) * rows : (3 + part) * rows]
+            merged = jnp.where(low, one, two)
+            for tile in range(lanes // 128):
+                start = (tile * 2 + part) * rows * deep + first + inner
+                kept[pl.ds(start, rows, stride=deep), :] = merged[:, tile * 128 : tile * 128 + 128]
 
     @pl.when(pl.program_id(0) == pl.num_programs(0) - 1)
     def regroup():
         chunk = lax.broadcasted_iota(jnp.int32, (half, 128), 1) // lat
         for tile in range(lanes // 128):
-            for spare in range(rows, kept_rows):
-                kept[pl.ds((tile * kept_rows + spare) * deep, half), :] = order_ref[:, :128] * 0.0
-
             def one_group(group, carry):
                 for part in range(2):
                     planes = []
                     for spot in range(pack):
-                        row = tile * kept_rows + (group * pack + spot) * 2 + part
+                        row = (tile * 2 + part) * rows + group * pack + spot
                         planes.append(kept[pl.ds(pl.multiple_of(row * deep, 8), half), :])
                     gap = 1
                     while gap < pack:
@@ -151,32 +155,36 @@
             lax.fori_loop(0, groups, one_group, 0)
 
 
-def synthesize(spectral, order_plane, cosine_row, diagonal_plane, lat):
-    pair, half, rows, degrees = spectral.shape
-    lanes = order_plane.shape[1]
+def synthesize(coefficients, order_plane, cosine_row, diagonal_plane, lat):
+    channels, _, _, degree_count = coefficients.shape
+    half, lanes = order_plane.shape
     block = 8
-    pitch = degrees + 8
-    pack = 128 // lat
-    groups = round_up(rows // 2, pack) // pack
+    tiles = round_up(degree_count, 128) // 128
+    rows = round_up(channels, 8)
+    tail = coefficients[..., (tiles - 1) * 128 :]
+    tail = jnp.pad(tail, ((0, 0), (0, 0), (0, 0), (0, tiles * 128 - degree_count)))
+    groups = round_up(channels, 128 // lat) // (128 // lat)
     out_dims = (lanes // 2 // lat, 2, 2, half, groups * 128)
-    kept_rows = lanes // 128 * groups * pack * 2 * (half + 8)
     return pl.pallas_call(
-        functools.partial(synthesis_kernel, block, pitch, lat),
+        functools.partial(synthesis_kernel, block, lat),
         grid=(half // block,),
         out_shape=jax.ShapeDtypeStruct(out_dims, jnp.bfloat16),
         in_specs=[
             pl.BlockSpec((half, lanes), lambda i: (0, 0)),
             pl.BlockSpec((1, lanes), lambda i: (0, 0)),
             pl.BlockSpec((half, lanes), lambda i: (0, 0)),
-            pl.BlockSpec((pair, block, rows, degrees), lambda i: (0, i, 0, 0)),
+            pl.BlockSpec(memory_space=pl.ANY),
+            pl.BlockSpec(memory_space=pl.ANY),
         ],
         out_specs=pl.BlockSpec(out_dims, lambda i: (0, 0, 0, 0, 0)),
         scratch_shapes=[
-            pltpu.VMEM((lanes // 128 * half * pitch, 128), jnp.float32),
-            pltpu.VMEM((kept_rows, 128), jnp.float32),
+            pltpu.VMEM((lanes // 128 * half * (tiles * 128 + 8), 128), jnp.float32),
+            pltpu.VMEM((lanes // 128 * 2 * rows * (half + 8), 128), jnp.float32),
+            pltpu.VMEM((4 * block, rows, tiles, 2, 128), jnp.int32),
+            pltpu.SemaphoreType.DMA((4 * block, tiles)),
         ],
         compiler_params=pltpu.CompilerParams(vmem_limit_bytes=60 * 1024 * 1024),
-    )(order_plane, cosine_row, diagonal_plane, spectral)
+    )(order_plane, cosine_row, diagonal_plane, coefficients, tail)
 
 
 def exchange_kernel(parts, sent, out, raw, near, sums, lower, other, total, *sems):
@@ -362,6 +370,33 @@
     )(found)
 
 
+def basis_kernel(fine_cos, fine_sin, coarse_cos, coarse_sin, out):
+    lon_count = out.shape[-1]
+    for high in range(2):
+        cos_b, sin_b = fine_cos[0, high], fine_sin[0, high]
+        for start in range(0, lon_count, 128):
+            tile = start // 128
+            width = min(128, lon_count - start)
+            cos_a = coarse_cos[0, high, :, tile : tile + 1]
+            sin_a = coarse_sin[0, high, :, tile : tile + 1]
+            real = (cos_a * cos_b - sin_a * sin_b).astype(jnp.bfloat16)
+            imag = (sin_a * cos_b + cos_a * sin_b).astype(jnp.bfloat16)
+            out[0, high, 0, :, start : start + width] = real[:, :width]
+            out[0, high, 1, :, start : start + width] = imag[:, :width]
+
+
+def make_basis(fine_cos, fine_sin, coarse_cos, coarse_sin, lon_count):
+    bands, _, half, lanes = fine_cos.shape
+    spec = pl.BlockSpec((1, 2, half, lanes), lambda i: (i, 0, 0, 0))
+    return pl.pallas_call(
+        basis_kernel,
+        grid=(bands,),
+        out_shape=jax.ShapeDtypeStruct((bands, 2, 2, half, lon_count), jnp.bfloat16),
+        in_specs=[spec] * 4,
+        out_specs=pl.BlockSpec((1, 2, 2, half, lon_count), lambda i: (i, 0, 0, 0, 0)),
+    )(fine_cos, fine_sin, coarse_cos, coarse_sin)
+
+
 def local(weather, coefficients, channel_scale):
     group_count = lax.axis_size("member")
     band_count = lax.axis_size("space")
@@ -371,10 +406,8 @@
     order_count = order_local * band_count
     lat_count = rows_local * band_count
     member_count = member_local * group_count
-    rows = member_local * channels * 2
     half = round_up(order_local, 16) // 2
     padded = 2 * half
-    degrees_padded = round_up(degree_count, 128)
 
     first_order = lax.axis_index("space") * order_local
     slots = jnp.arange(padded, dtype=jnp.int32)
@@ -400,10 +433,9 @@
     order_plane = pair_up(jnp.broadcast_to(order_values, (padded, lat_count)))
     cosine_row = jnp.tile(jnp.cos(colatitude), 2)[None, :]
 
-    spectral = turn_spectral(
-        coefficients.reshape(rows, order_local, degree_count), padded, degrees_padded, degree_count
-    ).reshape(2, half, rows, degrees_padded)
-    found = synthesize(spectral, order_plane, cosine_row, pair_up(diagonal), rows_local)
+    turned = coefficients.transpose(0, 1, 3, 2, 4)
+    turned = turned.reshape(member_local * channels, order_local, 2, degree_count)
+    found = synthesize(turned, order_plane, cosine_row, pair_up(diagonal), rows_local)
     depth = padded * 2
     flat = member_local * channels * rows_local
     found = found.reshape(band_count, depth, -1)
@@ -413,16 +445,20 @@
     slot = slots.reshape(2, half)
     row_order = band * order_local + slots[None, :]
     real_slot = jnp.broadcast_to(slots[None, :] < order_local, row_order.shape)
-    columns = jnp.arange(lon_count, dtype=jnp.int32)
-    phases = row_order[:, :, None] * columns % lon_count
-    angles = 2.0 * math.pi / lon_count * phases.astype(jnp.float32)
     weights = jnp.where(real_slot, jnp.where(row_order == 0, 1.0, math.sqrt(2.0)), 0.0)
     weights = weights.astype(jnp.float32)[:, :, None]
-    shape = (band_count, 2, half, lon_count)
-    basis = jnp.stack(
-        [(weights * jnp.cos(angles)).reshape(shape), (weights * jnp.sin(angles)).reshape(shape)], axis=2
-    ).astype(jnp.bfloat16)
-    basis = basis.reshape(band_count * depth, lon_count)
+
+    def waves(steps):
+        phases = row_order[:, :, None] * steps % lon_count
+        angles = 2.0 * math.pi / lon_count * phases.astype(jnp.float32)
+        shape = (band_count, 2, half, 128)
+        return jnp.cos(angles).reshape(shape), jnp.sin(angles).reshape(shape)
+
+    lanes = jnp.arange(128, dtype=jnp.int32)
+    fine = waves(lanes)
+    heavy = jnp.broadcast_to(weights, (band_count, padded, 128)).reshape(band_count, 2, half, 128)
+    coarse = [heavy * wave for wave in waves(lanes * 128 % lon_count)]
+    basis = make_basis(*fine, *coarse, lon_count).reshape(band_count * depth, lon_count)
 
     centred = centred.reshape(band_count * depth, -1)[:, :flat]
     noise = lax.dot_general(

time: 144 us -> 122 us (0.85)
  Pallas kernels: 101 us -> 89 us
  other arithmetic: 12.6 us -> 4.42 us
  local copies, waits for them, and re-layouts: 25 us -> 21.1 us
  matrix products: 5.09 us -> 7.15 us
    unnamed x7 -> x4, local copies, waits for them, and re-layouts: 19.7 us -> 0.01 us
    pallas_call x2, Pallas kernels: 37.9 us -> 25.8 us  [the longest x1 21.6 us: synthesize(): pl.pallas_call(functools.partial(synthesis_kernel, block, lat), grid=(hal...]
    another operation x5 -> x3, other arithmetic: 11.3 us -> 0.42 us
    pad x0 -> x1, local copies, waits for them, and re-layouts: none -> 8.98 us  [synthesize(): jnp.pad(tail, ((0, 0), (0, 0), (0, 0), (0, tiles * 128 - degree_count)))]
    slice x1 -> x2, local copies, waits for them, and re-layouts: 0.07 us -> 6.99 us  [the longest x1 6.92 us: synthesize(): tail = coefficients[..., (tiles - 1) * 128:]]
    mul x0 -> x1, other arithmetic: none -> 2.73 us  [local(): coarse = [heavy * wave for wave in waves(lanes * 128 % lon_count)]]
    dot_general x1, matrix products: 5.09 us -> 7.15 us  [local(): lax.dot_general(centred, basis, (((0,), (0,)), ((), ())), preferred_eleme...]
where the time goes in v3:
time: 122 us
  Pallas kernels  89 us (73%)
  local copies, waits for them, and re-layouts  21.1 us (17%)
  matrix products  7.15 us (6%)
  other arithmetic  4.42 us (4%)
    pallas_call x1, Pallas kernels, exchange(): pl.pallas_call(functools.partial(exchange_kernel, parts), out_shape=jax.S...  63.2 us
    pallas_call x1, Pallas kernels, synthesize(): pl.pallas_call(functools.partial(synthesis_kernel, block, lat), grid=(hal...  21.6 us
    pad x1, local copies, waits for them, and re-layouts, synthesize(): jnp.pad(tail, ((0, 0), (0, 0), (0, 0), (0, tiles * 128 - degree_count)))  8.98 us
    dot_general x1, matrix products, local(): lax.dot_general(centred, basis, (((0,), (0,)), ((), ())), preferred_eleme...  7.15 us
    slice x1, local copies, waits for them, and re-layouts, synthesize(): tail = coefficients[..., (tiles - 1) * 128:]  6.92 us
    pallas_call x1, Pallas kernels, make_basis(): pl.pallas_call(basis_kernel, grid=(bands,), out_shape=jax.ShapeDtypeStruc...  4.22 us
    dot_general x2, local copies, waits for them, and re-layouts, local(): lax.dot_general(centred, basis, (((0,), (0,)), ((), ())), preferred_eleme...  4.11 us
    mul x1, other arithmetic, local(): coarse = [heavy * wave for wave in waves(lanes * 128 % lon_count)]  2.73 us

profile of v3, /device:TPU:0, one launch (start us, length us, event | category | flops | bytes accessed | tf_op | source)
XLA Modules:
  0.0 121.8 jit_solution(3257478708085874229)
XLA Ops:
  0.0 0.3 reduce-window.9
  0.3 0.1 slice.40
  0.4 0.1 slice_reduce_fusion
  0.6 0.1 add_bitcast_fusion
  0.6 0.1 select_maximum_fusion
  0.7 0.1 dynamic-slice_add_fusion
  0.9 0.1 add_exponential_fusion
  1.0 0.1 slice_bitcast_fusion.2
  1.1 0.1 broadcast_in_dim.26
  1.1 0.1 broadcast_in_dim.48
  1.2 0.7 pad_maximum_fusion
  1.9 6.9 %slice.49 = s32[84,91,2,105]{3,2,1,0:T(2,128)} slice(s32[84,91,2,361]{3,2,1,0:T(2,128)} %bitcast.26), slice={[0:84], [0:91], [0:2], [256:361]} | slice | bytes 12841920 | tf_op jit(solution)/shard_map/slice | solution.py:164
  8.8 9.0 %pad.13.tail = s32[84,91,2,128]{3,2,1,0:T(2,128)} pad(s32[84,91,2,105]{3,2,1,0:T(2,128)} %slice.49, s32[]{:T(128)} %constant.62.clone.1), padding=0_0x0_0x0_0x0_23 | pad | bytes 14248420 | tf_op jit(solution)/shard_map/jit(_pad)/pad | solution.py:165
  17.9 0.6 broadcast_in_dim_tile.3.cosine_ref
  18.5 21.6 %shard_map.37 = bf16[4,2,2,48,1408]{4,3,2,1,0:T(8,128)(2,1)} custom-call(f32[48,128]{1,0:T(8,128)} %get-tuple-element.13.order_ref, f32[1,128]{1,0:T(1,128)} %broadcast_in_dim_tile.3.cosine_ref, f32[48,128]{1,0:T(8,128)} %get-tuple-element.14.diagonal_ref, s32[84,91,2,361]{3,2,1,0:T(2,128)} %bitcast.27, s32[84,91,2,128]{3,2,1,0:T(2,128)} %pad.13.tail), custom_call_target="tpu_custom_call" | custom-call | tf_op jit(solution)/shard_map/pallas_call | solution.py:168
  40.1 63.2 %shard_map.38 = bf16[4,192,1408]{2,1,0:T(8,128)(2,1)} custom-call(bf16[4,192,1408]{2,1,0:T(8,128)(2,1)} %bitcast.29), custom_call_target="tpu_custom_call" | custom-call | tf_op jit(solution)/shard_map/pallas_call | solution.py:351
  103.3 1.8 %slice_bitcast_fusion = bf16[1344,768]{0,1:T(8,128)(2,1)S(1)} fusion(bf16[768,1408]{1,0:T(8,128)(2,1)} %bitcast.28), kind=kLoop, calls=%fused_computation.2 | loop fusion | bytes 4128768 | tf_op jit(solution)/shard_map/dot_general | solution.py:464
  105.1 2.3 %copy.6 = bf16[1344,768]{1,0:T(8,128)(2,1)} copy(bf16[1344,768]{0,1:T(8,128)(2,1)S(1)} %slice_bitcast_fusion) | data formatting | bytes 4128768 | tf_op jit(solution)/shard_map/dot_general | solution.py:464
  107.4 0.0 copy-start
  107.5 0.0 copy-start.1
  107.5 0.1 fusion.13
  107.6 0.1 broadcast_add_fusion
  107.6 2.7 %sine_multiply_fusion = (f32[4,2,48,128]{3,2,1,0:T(8,128)}, f32[4,2,48,128]{3,2,1,0:T(8,128)}, f32[4,2,48,128]{3,2,1,0:T(8,128)}, f32[4,2,48,128]{3,2,1,0:T(8,128)}) fusion(s32[128]{0:T(128)S(1)} %and_select_fusion, f32[4,2,48]{2,1,0:T(2,128)S(1)} %fusion.13, s32[4,2,48]{2,1,0:T(2,128)S(1)} %broadcast_add_fusion), kind=kLoop, calls=%fused_computation.9 | loop fusion | flops 983040 | bytes 790016 | tf_op jit(solution)/shard_map/mul | solution.py:460
  110.4 4.2 %shard_map.39 = bf16[4,2,2,48,1440]{4,3,2,1,0:T(8,128)(2,1)} custom-call(f32[4,2,48,128]{3,2,1,0:T(8,128)} %get-tuple-element.9.fine_cos, f32[4,2,48,128]{3,2,1,0:T(8,128)} %get-tuple-element.10.fine_sin, f32[4,2,48,128]{3,2,1,0:T(8,128)} %get-tuple-element.8.coarse_cos, f32[4,2,48,128]{3,2,1,0:T(8,128)} %get-tuple-element.7.coarse_sin), custom_call_target="tpu_custom_call" | custom-call | tf_op jit(solution)/shard_map/pallas_call | solution.py:391
  114.6 0.0 copy-done
  114.6 0.0 copy-done.1
  114.6 7.2 %fusion = bf16[1,84,16,1440]{3,2,1,0:T(8,128)(2,1)} fusion(bf16[1,84,16,1440]{3,2,1,0:T(8,128)(2,1)} %param.3, bf16[84,16,768]{2,1,0:T(8,128)(2,1)S(1)} %bitcast.31, bf16[768,1440,1]{1,0,2:T(8,128)(2,1)} %bitcast.30, f32[84]{0:T(128)S(1)} %copy-done.1), kind=kOutput, calls=%fused_computation.1 | convolution fusion | flops 2980454400 | bytes 12018000 | tf_op jit(solution)/shard_map/dot_general | solution.py:464
  (13 shorter events, 0.2 us)
Async XLA Ops:
  107.4 7.1 %copy-start = (bf16[1344,768]{1,0:T(8,128)(2,1)S(1)}, bf16[1344,768]{1,0:T(8,128)(2,1)}, u32[]{:S(2)}) copy-start(bf16[1344,768]{1,0:T(8,128)(2,1)} %copy.6) | copy-start | bytes 6193156
  107.5 7.1 %copy-start.1 = (f32[84]{0:T(128)S(1)}, f32[84]{0:T(128)}, u32[]{:S(2)}) copy-start(f32[84]{0:T(128)} %param.5) | copy-start | bytes 1012
